TPU v7x, 32 devices: a whole 2x2x4 slice. The times are simulated.
32 devices in a mesh: tm: 4 (over y, x), chan: 8 (over z, core).
Axes of the slice: x: 2, y: 2, z: 4, core: 2. Of those that a mesh axis runs over, the one named last changes fastest.
Arguments:
- voltages: bfloat16 [8, 4, 32768, 512], P(None, None, ('tm', 'chan')), may hold values from -6 to 6
- taps: float32 [4, 512], replicated, may hold values from -3 to 3
- busy_mask: int32 [512], replicated, may hold values from 0 to 1, as said below
- drift_low: int32 [512], replicated, may hold values from -16 to 1
Outputs:
- drift_power: float32 [8, 32, 16, 2048], P(None, 'chan', None, 'tm')
Inputs may be any that keep to these rules, and one draw needn't show every extreme that they name: `busy_mask`: exactly 32 entries are 1.
All inputs are finite; a program needn't handle non-finite values.
Results may differ from a plain program's by a relative error of at most 0.008.
Values may be sent and summed in bfloat16 or wider, within the bound.
A program may use at most 192 MiB of HBM per device.

v0:
```python
import math

import jax
import jax.numpy as jnp
import numpy as np
from jax import lax
from jax.experimental import pallas as pl
from jax.experimental.pallas import tpu as pltpu
from jax.sharding import PartitionSpec as P

FA = 32
FB = 64
TAPS = 4
NDRIFT = 16
DSPAN = 16
FSTEP = 4
CH_DEV = 1


def passed_along(block, axis, distance):
    devices = range(lax.axis_size(axis))
    route = [(i - distance, i) for i in devices if i - distance in devices]
    return lax.ppermute(block, axis, route)


def busy_index(busy_mask, busy_count):
    before = jnp.cumsum(busy_mask) - busy_mask
    slot_ids = jnp.arange(busy_count, dtype=jnp.int32)
    is_slot = (busy_mask[:, None] == 1) & (before[:, None] == slot_ids[None, :])
    positions = jnp.arange(busy_mask.shape[0], dtype=jnp.int32)
    return jnp.sum(jnp.where(is_slot, positions[:, None], 0), axis=0)


def real_dft(sample_pos, freq_ids, length):
    phase_index = sample_pos[:, None] * freq_ids[None, :] % length
    angles = phase_index.astype(jnp.float32) * (2.0 * math.pi / length)
    cosines = jnp.cos(angles)
    sine_table = jnp.sin(angles)
    upper = jnp.stack([cosines, -sine_table], axis=1)
    lower = jnp.stack([sine_table, cosines], axis=1)
    return jnp.stack([upper, lower], axis=0).astype(jnp.bfloat16)


def to_bfloat(values):
    return lax.optimization_barrier(values.astype(jnp.bfloat16)).astype(jnp.float32)


def detect_power(spectra):
    items, lanes, chan_rows, samples = spectra.shape
    step_count = samples // (FA * FB)
    shaped = spectra.reshape(items, 2, 2, chan_rows, step_count, FA, FB)
    short_ids = jnp.arange(FA, dtype=jnp.int32)
    long_ids = jnp.arange(FB, dtype=jnp.int32)
    first_pass = jnp.einsum(
        "xopctab,paqf->xoqctfb",
        shaped,
        real_dft(short_ids, short_ids, FA),
        preferred_element_type=jnp.float32,
    )
    twist = short_ids[:, None] * long_ids[None, :] % (FA * FB)
    twist_angles = twist.astype(jnp.float32) * (2.0 * math.pi / (FA * FB))
    twist_cos = jnp.cos(twist_angles)
    twist_sin = jnp.sin(twist_angles)
    real_part = first_pass[:, :, 0]
    imag_part = first_pass[:, :, 1]
    turned = jnp.stack(
        [
            real_part * twist_cos + imag_part * twist_sin,
            imag_part * twist_cos - real_part * twist_sin,
        ],
        axis=2,
    ).astype(jnp.bfloat16)
    second_pass = jnp.einsum(
        "xoqctfb,qbsg->xosctgf",
        turned,
        real_dft(long_ids, long_ids, FB),
        preferred_element_type=jnp.float32,
    )
    powers = jnp.sum(second_pass * second_pass, axis=(1, 2)) / (4.0 * FA * FB)
    return powers.reshape(items, chan_rows, step_count, FA * FB)


def drift_rows(step_rows, first_step, drift_rates, first_bin, bin_width, pad_width):
    padded = jnp.pad(step_rows, ((0, 0), (0, 0), (0, 0), (pad_width, pad_width)))
    chan_rows = step_rows.shape[1]
    rate_count = drift_rates.shape[1]
    running = jnp.zeros((step_rows.shape[0], chan_rows, rate_count, bin_width), jnp.float32)
    for row_index in range(step_rows.shape[2]):
        step_time = first_step + row_index
        power_row = padded[:, 0, row_index]
        windows = []
        for rate_pos in range(rate_count):
            start = pad_width + first_bin + drift_rates[0, rate_pos] * step_time
            windows.append(lax.dynamic_slice_in_dim(power_row, start, bin_width, 1))
        per_slot = [jnp.stack(windows, axis=1)]
        running = running + jnp.stack(per_slot, axis=1)
    return running


def slot_rates(slot_part, drift_low):
    one_hot = slot_part[:, None] == jnp.arange(drift_low.shape[0], dtype=jnp.int32)[None, :]
    low_rates = jnp.sum(jnp.where(one_hot, drift_low[None, :], 0), axis=1)
    return low_rates[:, None] + jnp.arange(NDRIFT, dtype=jnp.int32)[None, :]


def shards(voltages, taps, busy_mask, drift_low):
    tm_count = lax.axis_size("tm")
    chan_devices = lax.axis_size("chan")
    count_of_beams, lanes, spec_dev, chan_count = voltages.shape
    busy_count = CH_DEV * tm_count * chan_devices
    step_count = FSTEP * tm_count
    pad_width = DSPAN * (step_count - 1)
    slot_index = busy_index(busy_mask, busy_count)
    slot_order = (
        slot_index.reshape(chan_devices, tm_count, CH_DEV).transpose(1, 0, 2).reshape(busy_count)
    )
    coarse_dft = real_dft(jnp.arange(chan_count, dtype=jnp.int32), slot_order, chan_count)
    following = passed_along(voltages[:, :, : TAPS - 1], ("tm", "chan"), -1)
    extended = jnp.concatenate([voltages, following], axis=2)
    filtered = taps[0] * extended[:, :, 0:spec_dev]
    for tap_index in range(1, TAPS):
        filtered = filtered + taps[tap_index] * extended[:, :, tap_index : tap_index + spec_dev]
    filtered = filtered.astype(jnp.bfloat16).reshape(count_of_beams, 2, 2, spec_dev, chan_count)
    coarse = jnp.einsum(
        "bopsn,pnqr->boqrs", filtered, coarse_dft, preferred_element_type=jnp.float32
    )
    coarse = (
        (coarse * chan_count ** (-0.5))
        .astype(jnp.bfloat16)
        .reshape(count_of_beams, 4, busy_count, spec_dev)
    )
    arrived = lax.all_to_all(
        lax.all_to_all(coarse, "tm", split_axis=2, concat_axis=3, tiled=True),
        "chan",
        split_axis=2,
        concat_axis=3,
        tiled=True,
    )
    ordered = arrived.reshape(count_of_beams, 4, CH_DEV, chan_devices, tm_count, spec_dev)
    ordered = ordered.transpose(0, 1, 2, 4, 3, 5).reshape(
        count_of_beams, 4, CH_DEV, tm_count * chan_devices * spec_dev
    )
    powers = detect_power(ordered)
    first_slot = lax.axis_index("chan") * (CH_DEV * tm_count) + lax.axis_index("tm") * CH_DEV
    drift_rates = slot_rates(lax.dynamic_slice_in_dim(slot_index, first_slot, CH_DEV), drift_low)
    drift_total = jnp.zeros((count_of_beams, CH_DEV, NDRIFT, FA * FB), jnp.float32)
    for group_index in range(tm_count):
        step_rows = powers[:, :, group_index * FSTEP : (group_index + 1) * FSTEP]
        drift_total = drift_total + to_bfloat(
            drift_rows(step_rows, group_index * FSTEP, drift_rates, 0, FA * FB, pad_width)
        )
    result = lax.all_to_all(
        (drift_total / step_count).astype(jnp.bfloat16),
        "tm",
        split_axis=3,
        concat_axis=1,
        tiled=True,
    ).astype(jnp.float32)
    return result


LANES = 128
FINE = FA * FB
SHORT = FINE // LANES
SLOTS = 32
HALO_ROWS = 8
PAD = 256
BLOCK = 256
DEPTH = 3
PITCH = 20


def short_dft(values, last=False):
    count = len(values)
    if count == 1:
        return values
    even = short_dft(values[0::2])
    odd = short_dft(values[1::2])
    low, high = [], []
    for k in range(count // 2):
        (same, turned), (term, flip) = even[k], odd[k]
        angle = 2.0 * math.pi * k / count
        if 4 * k == count:
            term, flip = flip, -term if not last else None
        elif k:
            cos, sin = math.cos(angle), math.sin(angle)
            term, flip = term * cos + flip * sin, flip * cos - term * sin if not last else None
        if last:
            low.append(same + term)
            high.append(same - term)
        else:
            low.append((same + term, turned + flip))
            high.append((same - term, turned - flip))
    return low + high


def first_block(part):
    return jnp.clip(2 * part - 1, 0, (FINE - 2 * PAD) // BLOCK - 2)


def flipped_bits(value, bits):
    moved, step = value, 1
    while step <= bits:
        if bits & step:
            moved = moved + step - 2 * step * lax.rem(value // step, 2)
        step *= 2
    return moved


def front_kernel(
    tm_count, chan_devices, volt, taps_hbm, mask_hbm, rate_hbm, trig_hbm, dft_hbm, tap_hbm, pick_hbm,
    out_ref, low_out, taps_ref, mask_ref, rate_ref, tap_ref, pick_ref, low_ref, vbuf, head, trig, dft, weight, edge, came_edge, g00, g01, g10, g11, spec, mid, power,
    send, held, volt_sem, const_sem, small_sem, edge_sem, swap_sent, swap_came, sent1, came1, sent2, came2, near_sem,
):
    beams, lanes, rows, chan_count = volt.shape
    items = beams // 2
    count = rows // SHORT
    tm, chan = lax.axis_index("tm"), lax.axis_index("chan")
    core = lax.rem(chan, 2)
    place = tm * chan_devices + chan
    last_place = tm_count * chan_devices - 1
    MESH = pl.DeviceIdType.MESH
    tm_peers = [flipped_bits(tm, q) for q in range(tm_count)]
    chan_peers = [flipped_bits(chan, k) for k in range(chan_devices)]
    far_first = range(chan_devices - 1, 0, -1)
    before = lax.rem(place + last_place, last_place + 1)
    after = lax.rem(place + 1, last_place + 1)
    before_id = (before // chan_devices, lax.rem(before, chan_devices))
    after_id = (after // chan_devices, lax.rem(after, chan_devices))

    barrier = pltpu.get_barrier_semaphore()
    for q in range(1, tm_count):
        pl.semaphore_signal(barrier, inc=1, device_id=(tm_peers[q], chan), device_id_type=MESH)
    for k in range(1, chan_devices):
        pl.semaphore_signal(barrier, inc=1, device_id=(tm, chan_peers[k]), device_id_type=MESH)
    pl.semaphore_signal(barrier, inc=1, device_id=before_id, device_id_type=MESH)
    pl.semaphore_signal(barrier, inc=1, device_id=after_id, device_id_type=MESH)

    def beam_of(i):
        return lax.rem(core + 1 + i, 2) * items + i // 2

    def volt_copy(i):
        slot = lax.rem(i, DEPTH)
        return pltpu.make_async_copy(volt.at[beam_of(i)], vbuf.at[slot], volt_sem.at[slot])

    trig_copy = pltpu.make_async_copy(trig_hbm, trig, const_sem.at[0])
    dft_copy = pltpu.make_async_copy(dft_hbm, dft, const_sem.at[1])
    head_copy = pltpu.make_async_copy(volt.at[:, :, pl.ds(0, HALO_ROWS), :], head, const_sem.at[2])
    smalls = [
        pltpu.make_async_copy(source, target, small_sem.at[n])
        for n, (source, target) in enumerate(
            ((mask_hbm, mask_ref), (rate_hbm, rate_ref), (taps_hbm, taps_ref), (tap_hbm, tap_ref), (pick_hbm, pick_ref))
        )
    ]
    for copy in smalls:
        copy.start()
    trig_copy.start()
    head_copy.start()
    volt_copy(0).start()
    for copy in smalls:
        copy.wait()

    square = (chan_count, chan_count)
    row = lax.broadcasted_iota(jnp.int32, square, 0)
    column = lax.broadcasted_iota(jnp.int32, square, 1)
    mask = mask_ref[...].astype(jnp.float32)
    counted = jnp.where(column < row, mask, jnp.where(column == row, (1.0 - mask) * chan_count, 0.0))
    ones = jnp.ones((chan_count, 2 * LANES), jnp.bfloat16)
    order = jnp.dot(counted.astype(jnp.bfloat16), ones, preferred_element_type=jnp.float32)
    lane = lax.broadcasted_iota(jnp.int32, (chan_count, 2 * LANES), 1)
    slot_of = lax.rem(lane, SLOTS).astype(jnp.float32)
    picked = jnp.where(order == slot_of, 1.0, 0.0).astype(jnp.bfloat16)
    low_ref[...] = jnp.dot(
        jnp.broadcast_to(rate_ref[...].astype(jnp.float32), (8, chan_count)).astype(jnp.bfloat16),
        picked[:, :LANES],
        preferred_element_type=jnp.float32,
    )
    low_copy = pltpu.make_async_copy(low_ref, low_out, small_sem.at[0])
    trig_copy.wait()
    cosines = jnp.dot(trig[0], picked, preferred_element_type=jnp.float32)
    sines = jnp.dot(trig[1], picked, preferred_element_type=jnp.float32)
    imag = lax.rem(lane // 64, 2) == 1
    upper = jnp.where(imag, -sines, cosines)
    lower = jnp.where(imag, cosines, sines)
    taps = taps_ref[...] * chan_count ** (-0.5)
    taps_high = taps.astype(jnp.bfloat16).astype(jnp.float32)
    taps_pair = jnp.concatenate([taps_high, taps - taps_high], axis=0).T.astype(jnp.bfloat16)
    for pol in range(2):
        factor = jnp.dot(taps_pair, tap_ref[pol], preferred_element_type=jnp.float32)
        weight[pol, :chan_count] = (upper * factor).astype(jnp.bfloat16)
        weight[pol, chan_count:] = (lower * factor).astype(jnp.bfloat16)
    volt_copy(1).start()
    dft_copy.start()
    low_copy.start()

    grams = ((g00, g01), (g10, g11))
    for left, right in grams:
        left[count * PITCH : count * PITCH + SHORT] = jnp.zeros((SHORT, LANES), jnp.float32)
        right[count * PITCH : count * PITCH + SHORT] = jnp.zeros((SHORT, LANES), jnp.float32)
    chunk = 256
    per_chunk = chunk // SHORT
    pol_of = lambda n: lax.rem(lax.broadcasted_iota(jnp.int32, (n, LANES), 1) // SLOTS, 2) == 0
    first_pol = pol_of(per_chunk)
    sign_of = lambda n: jnp.where(
        lax.broadcasted_iota(jnp.int32, (n, LANES), 1) < LANES // 2, 1.0, -1.0
    ).astype(jnp.float32)

    head_copy.wait()
    heads = beams * HALO_ROWS
    parts = []
    for pol in range(2):
        both_parts = [head[:, 2 * pol + p].reshape(heads, chan_count) for p in range(2)]
        parts.append(
            jnp.dot(jnp.concatenate(both_parts, axis=1), weight[pol], preferred_element_type=jnp.float32)
        )
    is_first = pol_of(heads)
    merged = lambda side: jnp.where(
        is_first, parts[0][:, side * LANES : (side + 1) * LANES], parts[1][:, side * LANES : (side + 1) * LANES]
    )
    moved = lambda side: jnp.where(
        is_first,
        pltpu.roll(parts[0][:, side * LANES : (side + 1) * LANES], LANES - SLOTS, 1),
        pltpu.roll(parts[1][:, side * LANES : (side + 1) * LANES], SLOTS, 1),
    )
    line = lax.rem(lax.broadcasted_iota(jnp.int32, (heads, LANES), 0), HALO_ROWS)
    edge[...] = (
        moved(1)
        + jnp.where(line >= 1, pltpu.roll(merged(1), 1, 0), 0.0)
        + jnp.where(line >= 2, pltpu.roll(moved(0), 2, 0), 0.0)
    )
    edge_copy = pltpu.make_async_remote_copy(
        src_ref=edge,
        dst_ref=came_edge,
        send_sem=edge_sem.at[0],
        recv_sem=edge_sem.at[1],
        device_id=before_id,
        device_id_type=MESH,
    )
    pl.semaphore_wait(barrier, tm_count + chan_devices)

    @pl.when(place > 0)
    def _():
        edge_copy.start()

    def matmuls(slot, start):
        for pol in range(2):
            left, right = grams[pol]
            part = jnp.dot(
                jnp.concatenate(
                    [vbuf[slot, 2 * pol, start : start + chunk], vbuf[slot, 2 * pol + 1, start : start + chunk]],
                    axis=1,
                ),
                weight[pol],
                preferred_element_type=jnp.float32,
            )
            for m in range(per_chunk):
                at = (start // SHORT + m) * PITCH
                left[at : at + SHORT] = part[m * SHORT : (m + 1) * SHORT, :LANES]
                right[at : at + SHORT] = part[m * SHORT : (m + 1) * SHORT, LANES:]

    def combine(i, start):
        def rows_at(at):
            return pl.ds((start // SHORT + at // SHORT) * PITCH + at % SHORT, per_chunk, stride=PITCH)

        def both(at):
            low, high = rows_at(at), rows_at(at + 2)
            return g00[low, :] + g01[high, :], g10[low, :] + g11[high, :]

        here = both(0)
        where = pl.ds(pl.multiple_of(core * count + start // SHORT, per_chunk), per_chunk)
        for at in range(SHORT):
            later = both(at + 1)
            value = jnp.where(
                first_pol,
                here[0] + pltpu.roll(later[0], LANES - SLOTS, 1),
                here[1] + pltpu.roll(later[1], SLOTS, 1),
            )
            spec[i, at, where, :] = value.astype(jnp.bfloat16)
            here = later

    def patch(i):
        where = pl.ds(pl.multiple_of(core * count + count - per_chunk, per_chunk), per_chunk)
        rows8 = came_edge[pl.ds(pl.multiple_of(beam_of(i) * HALO_ROWS, HALO_ROWS), HALO_ROWS), :]
        final = lax.broadcasted_iota(jnp.int32, (per_chunk, LANES), 0) == per_chunk - 1
        for n in range(TAPS - 1):
            at = SHORT - TAPS + 1 + n
            more = jnp.where(final, jnp.broadcast_to(rows8[n : n + 1], (per_chunk, LANES)), 0.0)
            spec[i, at, where, :] = (spec[i, at, where, :].astype(jnp.float32) + more).astype(jnp.bfloat16)

    def swap(i):
        half = pl.ds(pl.multiple_of(core * count, count), count)
        return pltpu.make_async_remote_copy(
            src_ref=spec.at[i, :, half, :],
            dst_ref=spec.at[i + 1, :, half, :],
            send_sem=swap_sent.at[i // 2],
            recv_sem=swap_came.at[i // 2],
            device_id=(tm, chan + 1 - 2 * core),
            device_id_type=MESH,
        )

    def fine_first(i):
        sign_full = sign_of(LANES).astype(jnp.bfloat16)
        for at in range(SHORT):
            plain = spec[i, at]
            flipped = pltpu.roll(plain, LANES // 2, 1) * sign_full
            mid[at, :LANES] = jnp.dot(
                dft[at],
                jnp.concatenate(
                    [jnp.concatenate([plain, flipped], axis=0), jnp.concatenate([flipped, -plain], axis=0)], axis=1
                ),
                preferred_element_type=jnp.float32,
            )

    def fine_second(at_row):
        rows8 = pl.ds(at_row, 8)
        spectra = short_dft([(mid[at, rows8, :LANES], mid[at, rows8, LANES:]) for at in range(SHORT)], True)
        for high, value in enumerate(spectra):
            where = pl.ds(high // 2 * LANES + at_row, 8)
            power[where, high % 2 * LANES : (high % 2 + 1) * LANES] = (value * value).astype(jnp.bfloat16)

    def fine_last(item):
        for pair in range(FINE // BLOCK // 2):
            sums = lax.dot_general(
                pick_ref[...],
                power[pair * BLOCK : (pair + 1) * BLOCK, :],
                (((1,), (1,)), ((), ())),
                preferred_element_type=jnp.float32,
            )
            for group in range(chan_devices):
                for side in range(2):
                    send[item, group, 2 * pair + side] = sums[
                        group * 8 : group * 8 + 8, side * LANES : (side + 1) * LANES
                    ].astype(jnp.bfloat16)

    def along_chan(item, k):
        return pltpu.make_async_remote_copy(
            src_ref=send.at[item, chan_peers[k]],
            dst_ref=held.at[item, k],
            send_sem=sent1.at[item, k],
            recv_sem=came1.at[item, k],
            device_id=(tm, chan_peers[k]),
            device_id_type=MESH,
        )

    def along_tm(item, k, q):
        block = held.at[item, k] if k else send.at[item, chan]
        return pltpu.make_async_remote_copy(
            src_ref=block.at[pl.ds(first_block(tm_peers[q]), 4)],
            dst_ref=out_ref.at[tm, chan_peers[k], item],
            send_sem=sent2.at[item, k, q],
            recv_sem=came2.at[item, k, q],
            device_id=(tm_peers[q], chan),
            device_id_type=MESH,
        )

    def near_copy(item, k):
        block = held.at[item, k] if k else send.at[item, chan]
        return pltpu.make_async_copy(
            block.at[pl.ds(first_block(tm), 4)], out_ref.at[tm, chan_peers[k], item], near_sem.at[item, k]
        )

    def forward(item):
        for k in range(chan_devices):
            if k:
                along_chan(item, k).wait_recv()
            for q in range(tm_count - 1, 0, -1):
                along_tm(item, k, q).start()
            near_copy(item, k).start()

    def coarse_start(i):
        volt_copy(i).wait()

        @pl.when(i + 2 < beams)
        def _():
            volt_copy(i + 2).start()

    def coarse_rest(i):
        for start in range(chunk, rows, chunk):
            matmuls(lax.rem(i, DEPTH), start)
            combine(i, start - chunk)

    def share(item):
        for k in far_first:
            along_chan(item, k).start()

        @pl.when(item > 0)
        def _():
            forward(item - 1)

    @pl.loop(0, items)
    def _(pair):
        i = 2 * pair
        done = jnp.maximum(i - 1, 0)
        item = jnp.maximum(pair - 1, 0)
        coarse_start(i)
        matmuls(lax.rem(i, DEPTH), 0)
        combine(done, rows - chunk)

        @pl.when(pair == 0)
        def _():
            coarse_rest(i)

        @pl.when(pair > 0)
        def _():
            @pl.when(pair == 1)
            def _():
                dft_copy.wait()

            patch(i - 1)
            swap(i - 2).wait_recv()
            fine_first(done)
            groups = list(range(0, LANES, 8))
            for start in range(chunk, rows, chunk):
                matmuls(lax.rem(i, DEPTH), start)
                combine(i, start - chunk)
                share_of = len(groups) // ((rows - start) // chunk)
                for at_row in groups[:share_of]:
                    fine_second(at_row)
                groups = groups[share_of:]
            fine_last(item)
            share(item)

        coarse_start(i + 1)
        matmuls(lax.rem(i + 1, DEPTH), 0)
        combine(i, rows - chunk)

        @pl.when(pair == 0)
        def _():
            @pl.when(place < last_place)
            def _():
                edge_copy.wait_recv()

            @pl.when(place == last_place)
            def _():
                came_edge[...] = jnp.zeros_like(came_edge)

        patch(i)
        swap(i).start()
        coarse_rest(i + 1)

    combine(beams - 1, rows - chunk)
    patch(beams - 1)
    swap(beams - 2).wait_recv()
    fine_first(beams - 1)

    for at_row in range(0, LANES, 8):
        fine_second(at_row)
    fine_last(items - 1)
    share(items - 1)
    forward(items - 1)

    low_copy.wait()

    @pl.when(place > 0)
    def _():
        edge_copy.wait_send()

    @pl.loop(0, items)
    def _(item):
        swap(2 * item).wait_send()
        for k in range(chan_devices):
            if k:
                along_chan(item, k).wait_send()
            for q in range(1, tm_count):
                along_tm(item, k, q).wait_send()
            near_copy(item, k).wait()
        for k in range(chan_devices):
            for q in range(1, tm_count):
                pltpu.make_async_remote_copy(
                    src_ref=held.at[item, k, pl.ds(0, 4)],
                    dst_ref=out_ref.at[tm_peers[q], chan_peers[k], item],
                    send_sem=sent2.at[item, k, q],
                    recv_sem=came2.at[item, k, q],
                    device_id=(tm_peers[q], chan),
                    device_id_type=MESH,
                ).wait_recv()


def front(voltages, taps, busy_mask, drift_low, tm_count, chan_devices):
    beams, lanes, rows, chan_count = voltages.shape
    items = beams // 2
    ids = np.arange(chan_count)
    angles = (ids[:, None] * ids[None, :] % chan_count) * (2.0 * math.pi / chan_count)
    trig = jnp.asarray(np.stack([np.cos(angles), np.sin(angles)]), jnp.bfloat16)
    position = np.arange(SHORT)[:, None, None] + SHORT * np.arange(LANES)[None, None, :]
    turns = (position * np.arange(LANES)[None, :, None] % FINE) * (2.0 * math.pi / FINE)
    dft = jnp.asarray(np.concatenate([np.cos(turns), np.sin(turns)], axis=2), jnp.bfloat16)
    column = np.arange(2 * LANES)
    tap_of = np.stack([2 * (column // LANES) + (column // SLOTS % 2 ^ pol) for pol in range(2)])
    tap_pick = tap_of[:, None, :] == (np.arange(2 * TAPS) % TAPS)[None, :, None]
    per_group = SLOTS // chan_devices
    line = np.arange(8 * chan_devices)
    group, side, slot = line // 8, line % 8 // per_group, line % per_group
    lane = np.arange(2 * LANES)
    pick = (side[:, None] == lane[None, :] // LANES) & (
        (group * per_group + slot)[:, None] == lane[None, :] % SLOTS
    )
    hbm = pl.BlockSpec(memory_space=pl.ANY)
    dma = pltpu.SemaphoreType.DMA
    kernel = lambda *refs: front_kernel(tm_count, chan_devices, *refs)
    blocks = FINE // BLOCK
    gram = pltpu.VMEM(((rows // SHORT + 1) * PITCH, LANES), jnp.float32)
    return pl.pallas_call(
        kernel,
        in_specs=[hbm] * 8,
        out_specs=(hbm, hbm),
        out_shape=(
            jax.ShapeDtypeStruct((tm_count, chan_devices, items, 4, 8, LANES), jnp.bfloat16),
            jax.ShapeDtypeStruct((8, LANES), jnp.float32),
        ),
        scratch_shapes=[
            pltpu.VMEM(taps.shape, jnp.float32),
            pltpu.VMEM((1, chan_count), jnp.int32),
            pltpu.VMEM((1, chan_count), jnp.int32),
            pltpu.VMEM(tap_pick.shape, jnp.bfloat16),
            pltpu.VMEM(pick.shape, jnp.bfloat16),
            pltpu.VMEM((8, LANES), jnp.float32),
            pltpu.VMEM((DEPTH, lanes, rows, chan_count), jnp.bfloat16),
            pltpu.VMEM((beams, lanes, HALO_ROWS, chan_count), jnp.bfloat16),
            pltpu.VMEM(trig.shape, jnp.bfloat16),
            pltpu.VMEM(dft.shape, jnp.bfloat16),
            pltpu.VMEM((2, 2 * chan_count, 2 * LANES), jnp.bfloat16),
            pltpu.VMEM((beams * HALO_ROWS, LANES), jnp.float32),
            pltpu.VMEM((beams * HALO_ROWS, LANES), jnp.float32),
            gram,
            gram,
            gram,
            gram,
            pltpu.VMEM((beams, SHORT, LANES, LANES), jnp.bfloat16),
            pltpu.VMEM((SHORT, LANES + 8, 2 * LANES), jnp.float32),
            pltpu.VMEM((FINE // 2, 2 * LANES), jnp.bfloat16),
            pltpu.VMEM((items, chan_devices, blocks, 8, LANES), jnp.bfloat16),
            pltpu.VMEM((items, chan_devices, blocks, 8, LANES), jnp.bfloat16),
            dma((DEPTH,)),
            dma((3,)),
            dma((5,)),
            dma((2,)),
            dma((items,)),
            dma((items,)),
            dma((items, chan_devices)),
            dma((items, chan_devices)),
            dma((items, chan_devices, tm_count)),
            dma((items, chan_devices, tm_count)),
            dma((items, chan_devices)),
        ],
        compiler_params=pltpu.CompilerParams(
            collective_id=0, has_side_effects=True, vmem_limit_bytes=56 * 2**20
        ),
    )(
        voltages,
        taps,
        busy_mask.reshape(1, chan_count),
        drift_low.reshape(1, chan_count),
        trig,
        dft,
        jnp.asarray(tap_pick, jnp.bfloat16),
        jnp.asarray(pick, jnp.bfloat16),
    )


STRIDE = 40


def drift_kernel(scale, low_hbm, in_hbm, out_ref, low_ref, in_ref, rows_ref, stage_ref, sems):
    steps, beams, tiles, _, _ = in_ref.shape
    _, _, rates, width = out_ref.shape
    slots = rows_ref.shape[0]
    pad = PAD // LANES
    wide = 2 * tiles
    slot = pl.program_id(0)
    tm, chan = lax.axis_index("tm"), lax.axis_index("chan")
    parts = 4
    portion = steps // parts

    def arrival(n):
        span = pl.ds(n * portion, portion)
        return pltpu.make_async_copy(in_hbm.at[span], in_ref.at[span], sems.at[n])

    @pl.when(slot == 0)
    def _():
        low_copy = pltpu.make_async_copy(low_hbm, low_ref, sems.at[parts])
        for n in range(parts):
            arrival(n).start()
        low_copy.start()
        empty = jnp.zeros((beams, LANES), jnp.float32)

        @pl.loop(0, parts)
        def _(n):
            arrival(n).wait()

            @pl.loop(0, portion)
            def _(step):
                t = n * portion + step
                for beam in range(beams):
                    stage_ref[beam * STRIDE : beam * STRIDE + 8 * tiles] = (
                        in_ref[t, beam].astype(jnp.float32).reshape(8 * tiles, LANES)
                    )
                for at in range(slots):
                    rows = [empty] * pad
                    rows += [stage_ref[pl.ds(tile * slots + at, beams, stride=STRIDE), :] for tile in range(wide)]
                    rows += [empty] * pad
                    for tile in range(wide + 2 * pad - 2):
                        rows_ref[at, t, tile] = jnp.concatenate([rows[tile], rows[tile + 2]], axis=0).astype(
                            jnp.bfloat16
                        )

        low_copy.wait()

    lane8 = lax.broadcasted_iota(jnp.int32, (8, LANES), 1)
    low = jnp.sum(jnp.where(lane8 == chan * slots + slot, low_ref[...], 0.0)[:1]).astype(jnp.int32)
    lane = lax.broadcasted_iota(jnp.int32, (2 * beams, LANES), 1)
    origin = tm * width - BLOCK * first_block(tm) + PAD
    for rate in range(rates):
        totals = None
        for t in range(steps):
            start = (low * t + origin) + rate * t
            base = lax.shift_right_logical(start, 7)
            if t:
                rest = start & (LANES - 1)
                back = (LANES - rest) & (LANES - 1)
                keep = lane >= rest
                three = rows_ref[slot, t, pl.ds(base, 3)]
                even, odd = [
                    pltpu.roll(jnp.where(keep, three[k], three[k + 1]), back, 1).astype(jnp.float32) for k in range(2)
                ]
            else:
                two = rows_ref[slot, t, pl.ds(base, 2)]
                even, odd = two[0].astype(jnp.float32), two[1].astype(jnp.float32)
            added = [even[:beams], odd[:beams], even[beams:], odd[beams:]]
            totals = added if totals is None else [total + more for total, more in zip(totals, added)]
        out_ref[:, 0, rate, :] = jnp.concatenate(totals, axis=1) * scale


def drift_sums(arrived, low_rates, slots, width):
    steps, beams, tiles, _, _ = arrived.shape
    kernel = lambda *refs: drift_kernel(1.0 / (4.0 * FINE * steps), *refs)
    hbm = pl.BlockSpec(memory_space=pl.ANY)
    return pl.pallas_call(
        kernel,
        grid=(slots,),
        in_specs=[hbm, hbm],
        out_specs=pl.BlockSpec((beams, 1, NDRIFT, width), lambda s: (0, s, 0, 0)),
        out_shape=jax.ShapeDtypeStruct((beams, slots, NDRIFT, width), jnp.float32),
        scratch_shapes=[
            pltpu.VMEM((8, LANES), jnp.float32),
            pltpu.VMEM(arrived.shape, jnp.bfloat16),
            pltpu.VMEM((slots, steps, 2 * tiles + 2 * PAD // LANES - 2, 2 * beams, LANES), jnp.bfloat16),
            pltpu.VMEM((beams * STRIDE, LANES), jnp.float32),
            pltpu.SemaphoreType.DMA((5,)),
        ],
        compiler_params=pltpu.CompilerParams(vmem_limit_bytes=60 * 2**20),
    )(low_rates, arrived)


def paired_shards(voltages, taps, busy_mask, drift_low):
    tm_count = lax.axis_size("tm")
    chan_devices = lax.axis_size("chan")
    arrived, low_rates = front(voltages, taps, busy_mask, drift_low, tm_count, chan_devices)
    arrived = arrived.reshape(tm_count * chan_devices // 2, voltages.shape[0], 4, 8, LANES)
    return drift_sums(arrived, low_rates, SLOTS // chan_devices, FINE // tm_count)


def two_devices_hold_a_step(mesh, voltages):
    tm_count, chan_devices = mesh.shape["tm"], mesh.shape["chan"]
    rows = voltages.shape[2] // (tm_count * chan_devices)
    return (
        2 * rows == FINE
        and tm_count == 4
        and chan_devices == 2 * FSTEP
        and CH_DEV * tm_count * chan_devices == SLOTS
        and voltages.shape[0] == 8
        and PAD >= DSPAN * (FSTEP * tm_count - 1)
    )


def solution(mesh):
    in_specs = (P(None, None, ("tm", "chan"), None), P(), P(), P())
    out_specs = P(None, "chan", None, "tm")

    def run(voltages, taps, busy_mask, drift_low):
        body = paired_shards if two_devices_hold_a_step(mesh, voltages) else shards
        return jax.shard_map(
            body, mesh=mesh, in_specs=in_specs, out_specs=out_specs, check_vma=False
        )(voltages, taps, busy_mask, drift_low)

    return run
```

profile of v0, /device:TPU:0, one launch (start us, length us, event | category | flops | bytes accessed | tf_op | source)
XLA Modules:
  0.0 42.5 jit_solution(231220084003970511)
XLA Ops:
  0.0 36.4 %shard_map.82 = (bf16[4,8,4,4,8,128]{5,4,3,2,1,0:T(8,128)(2,1)}, f32[8,128]{1,0:T(8,128)}) custom-call(bf16[8,4,1024,512]{3,2,1,0:T(8,128)(2,1)} %refs_0_.1, f32[4,512]{1,0:T(4,128)} %refs_1_.1, s32[1,512]{1,0:T(1,128)} %bitcast.4, s32[1,512]{1,0:T(1,128)} %bitcast.5, bf16[2,512,512]{2,1,0:T(8,128)(2,1)} %constant.8.clone.refs_4_, ...), custom_call_target="tpu_custom_call" | custom-call | tf_op jit(solution)/shard_map/pallas_call | solution.py:603
  36.4 6.1 %shard_map.83 = f32[8,4,16,512]{3,2,1,0:T(8,128)} custom-call(f32[8,128]{1,0:T(8,128)} %get-tuple-element.7.refs_0_, bf16[16,8,4,8,128]{4,3,2,1,0:T(8,128)(2,1)} %bitcast.3), custom_call_target="tpu_custom_call" | custom-call | tf_op jit(solution)/shard_map/pallas_call | solution.py:738
where the time goes:
time: 42.6 us; the launch traced here: 42.5 us
  Pallas kernels  42.5 us (100%)
    pallas_call x1, Pallas kernels, front(): pl.pallas_call(kernel, in_specs=[hbm] * 8, out_specs=(hbm, hbm), out_shap...  36.4 us
    pallas_call x1, Pallas kernels, drift_sums(): pl.pallas_call(kernel, grid=(slots,), in_specs=[hbm, hbm], out_specs=pl.B...  6.05 us

commit v1 on v0

--- a/solution.py
+++ b/solution.py
@@ -688,16 +688,15 @@
         def _(n):
             arrival(n).wait()
 
-            @pl.loop(0, portion)
-            def _(step):
+            for step in range(portion):
                 t = n * portion + step
                 for beam in range(beams):
-                    stage_ref[beam * STRIDE : beam * STRIDE + 8 * tiles] = (
+                    stage_ref[step, beam * STRIDE : beam * STRIDE + 8 * tiles] = (
                         in_ref[t, beam].astype(jnp.float32).reshape(8 * tiles, LANES)
                     )
                 for at in range(slots):
                     rows = [empty] * pad
-                    rows += [stage_ref[pl.ds(tile * slots + at, beams, stride=STRIDE), :] for tile in range(wide)]
+                    rows += [stage_ref[step, pl.ds(tile * slots + at, beams, stride=STRIDE), :] for tile in range(wide)]
                     rows += [empty] * pad
                     for tile in range(wide + 2 * pad - 2):
                         rows_ref[at, t, tile] = jnp.concatenate([rows[tile], rows[tile + 2]], axis=0).astype(
@@ -745,7 +744,7 @@
             pltpu.VMEM((8, LANES), jnp.float32),
             pltpu.VMEM(arrived.shape, jnp.bfloat16),
             pltpu.VMEM((slots, steps, 2 * tiles + 2 * PAD // LANES - 2, 2 * beams, LANES), jnp.bfloat16),
-            pltpu.VMEM((beams * STRIDE, LANES), jnp.float32),
+            pltpu.VMEM((steps // 4, beams * STRIDE, LANES), jnp.float32),
             pltpu.SemaphoreType.DMA((5,)),
         ],
         compiler_params=pltpu.CompilerParams(vmem_limit_bytes=60 * 2**20),

time: 42.6 us -> 42.6 us (level)
  no operation moved by 1% of the time
where the time goes in v1:
time: 42.6 us; the launch traced here: 42.4 us
  Pallas kernels  42.4 us (100%)
    pallas_call x1, Pallas kernels, front(): pl.pallas_call(kernel, in_specs=[hbm] * 8, out_specs=(hbm, hbm), out_shap...  36.4 us
    pallas_call x1, Pallas kernels, drift_sums(): pl.pallas_call(kernel, grid=(slots,), in_specs=[hbm, hbm], out_specs=pl.B...  5.98 us

profile of v1, /device:TPU:0, one launch (start us, length us, event | category | flops | bytes accessed | tf_op | source)
XLA Modules:
  0.0 42.4 jit_solution(11330179489910683473)
XLA Ops:
  0.0 36.4 %shard_map.82 = (bf16[4,8,4,4,8,128]{5,4,3,2,1,0:T(8,128)(2,1)}, f32[8,128]{1,0:T(8,128)}) custom-call(bf16[8,4,1024,512]{3,2,1,0:T(8,128)(2,1)} %refs_0_.1, f32[4,512]{1,0:T(4,128)} %refs_1_.1, s32[1,512]{1,0:T(1,128)} %bitcast.4, s32[1,512]{1,0:T(1,128)} %bitcast.5, bf16[2,512,512]{2,1,0:T(8,128)(2,1)} %constant.8.clone.refs_4_, ...), custom_call_target="tpu_custom_call" | custom-call | tf_op jit(solution)/shard_map/pallas_call | solution.py:603
  36.4 6.0 %shard_map.83 = f32[8,4,16,512]{3,2,1,0:T(8,128)} custom-call(f32[8,128]{1,0:T(8,128)} %get-tuple-element.7.refs_0_, bf16[16,8,4,8,128]{4,3,2,1,0:T(8,128)(2,1)} %bitcast.3), custom_call_target="tpu_custom_call" | custom-call | tf_op jit(solution)/shard_map/pallas_call | solution.py:737
